TPU v7x, 32 devices: a whole 2x2x4 slice. The times are simulated.
32 devices in a mesh: row: 4 (over x, core), col: 8 (over z, y).
Axes of the slice: x: 2, y: 2, z: 4, core: 2. Of those that a mesh axis runs over, the one named last changes fastest.
Arguments:
- points: float32 [16, 8192], P(None, ('row', 'col')), may hold values from -6 to 6
- lengthscale: float32 [16], replicated, may hold values from 2 to 8
- signal: float32 [1], replicated, may hold values from 0.5 to 2
- noise: float32 [1], replicated, may hold values from 0.05 to 0.5
- targets: float32 [8192], P(('row', 'col')), may hold values from -12 to 12
- probe_bits: int32 [31, 8192], P(None, ('row', 'col')), may hold values from 0 to 1
Outputs:
- solution: float32 [32, 8192], P(None, ('row', 'col'))
- residual: float32 [32, 8192], P(None, ('row', 'col'))
All inputs are finite; a program needn't handle non-finite values.
Results may differ from a plain program's by a relative error of at most 0.0013.
Values sent between devices are 32-bit elements; how exact they have to be, the bound alone decides.
No kernel may reach another device: no remote copies, remote signals or barrier semaphores. Data moves between devices by JAX's collectives and lax.ppermute only.
A program may use at most 128 MiB of HBM per device.

v0:
```python
import jax
import jax.numpy as jnp
from jax import lax
from jax.sharding import PartitionSpec as P

ITERS = 3
ROOT_FIVE = 5.0**0.5


def matern_tile(row_scaled, col_scaled, signal_value):
    row_sq = jnp.sum(row_scaled * row_scaled, axis=0)
    col_sq = jnp.sum(col_scaled * col_scaled, axis=0)
    cross_term = lax.dot_general(
        row_scaled,
        col_scaled,
        (((0,), (0,)), ((), ())),
        precision=lax.Precision.HIGHEST,
        preferred_element_type=jnp.float32,
    )
    dist_sq = jnp.maximum(row_sq[:, None] + col_sq[None, :] - 2.0 * cross_term, 0.0)
    radius = jnp.sqrt(dist_sq)
    return (
        signal_value
        * (1.0 + ROOT_FIVE * radius + 5.0 / 3.0 * dist_sq)
        * jnp.exp(-ROOT_FIVE * radius)
    )


def row_blocks(row_scaled):
    row_total = row_scaled.shape[1]
    block_rows = min(1024, row_total)
    block_count = row_total // block_rows
    return row_scaled.reshape(row_scaled.shape[0], block_count, block_rows).transpose(1, 0, 2)


def apply_tile(row_scaled, col_scaled, signal_value, vectors):
    row_total = row_scaled.shape[1]
    stacked = row_blocks(row_scaled)

    def one_block(row_block):
        kernel_tile = matern_tile(row_block, col_scaled, signal_value)
        return lax.dot_general(
            vectors,
            kernel_tile,
            (((1,), (1,)), ((), ())),
            precision=lax.Precision.HIGHEST,
            preferred_element_type=jnp.float32,
        )

    pieces = lax.map(one_block, stacked)
    return pieces.transpose(1, 0, 2).reshape(vectors.shape[0], row_total)


def squares(residual):
    return lax.psum(jnp.sum(residual * residual, axis=1), ("row", "col"))


def body(points, lengthscale, signal, noise, targets, probe_bits):
    scaled = points / lengthscale[:, None]
    signs = 2.0 * probe_bits.astype(jnp.float32) - 1.0
    right_side = jnp.concatenate([targets[None, :], signs], axis=0)
    signal_value = signal[0]
    noise_value = noise[0]
    every_point = lax.all_gather(scaled, ("row", "col"), axis=1, tiled=True)
    solution = jnp.zeros_like(right_side)
    residual = right_side
    direction = right_side
    norm_now = squares(residual)
    for step in range(ITERS):
        summed = apply_tile(
            scaled,
            every_point,
            signal_value,
            lax.all_gather(direction, ("row", "col"), axis=1, tiled=True),
        )
        image = summed + noise_value * direction
        curved = lax.psum(jnp.sum(direction * image, axis=1), ("row", "col"))
        alpha = norm_now / curved
        solution = solution + alpha[:, None] * direction
        residual = residual - alpha[:, None] * image
        if step + 1 < ITERS:
            norm_next = squares(residual)
            direction = residual + (norm_next / norm_now)[:, None] * direction
            norm_now = norm_next
    return (solution, residual)


def solution(mesh):
    return jax.shard_map(
        body,
        mesh=mesh,
        in_specs=(
            P(None, ("row", "col")),
            P(),
            P(),
            P(),
            P(("row", "col")),
            P(None, ("row", "col")),
        ),
        out_specs=(P(None, ("row", "col")), P(None, ("row", "col"))),
        check_vma=False,
    )
```

profile of v0, /device:TPU:0, one launch (start us, length us, event | category | flops | bytes accessed | tf_op | source)
XLA Modules:
  0.0 442.8 jit_solution(3945853298160864915)
XLA Ops:
  7.2 0.0 all-gather.4.cloned.1.call-start
  7.2 0.8 multiply_add_fusion.3
  8.0 1.3 pad_maximum_fusion
  9.3 0.0 all-gather.4.cloned.1.call-update
  9.3 0.0 all-gather.6.cloned.1.call-start
  10.6 0.8 multiply_reduce_fusion.7
  11.5 73.2 %all_gather.13 = f32[16,8192]{1,0:T(8,128)S(1)} all-gather(f32[16,256]{1,0:T(8,128)S(1)} %get-tuple-element.51), channel_id=1, replica_groups=mesh['row'=4,'col'=8] {'row','col'}, dimensions={1}, use_global_device_ids=true | all-gather | bytes 540672 | tf_op jit(solution)/shard_map/all_gather | solution.py:64
  84.6 0.1 multiply_reduce_fusion
  84.7 0.0 copy-start.2
  84.7 14.0 %exponential_multiply_fusion = f32[256,8192]{1,0:T(8,128)} fusion(f32[16,256]{1,0:T(8,128)S(1)} %get-tuple-element.51, f32[16,8192]{1,0:T(8,128)S(1)} %all_gather.13, f32[8192]{0:T(1024)S(1)} %multiply_reduce_fusion, f32[256]{0:T(256)S(1)} %get-tuple-element.50, f32[]{:T(128)} %bitcast.11), kind=kOutput, calls=%fused_computation.3 | convolution fusion | flops 425721856 | bytes 8963076 | tf_op jit(solution)/shard_map/while/body/eval_jaxpr/dot_general | solution.py:13
  98.7 0.0 copy-start.3
  98.7 0.0 all-gather.4.cloned.1.call-done
  98.7 0.0 copy-done.2
  98.8 11.2 %multiply_reduce_fusion.5 = (f32[32]{0:T(128)S(1)}, f32[32]{0:T(128)S(1)}, f32[32,256]{1,0:T(8,128)S(1)}) fusion(f32[32,256]{1,0:T(8,128)S(1)} %copy-done.2, f32[]{:T(128)} %bitcast.12, f32[32,8192]{1,0:T(8,128)} %all-gather.4.cloned.1.call-done, f32[256,8192]{1,0:T(8,128)} %exponential_multiply_fusion), kind=kOutput, calls=%fused_computation.19 | convolution fusion | flops 805355456 | bytes 9502980 | tf_op jit(solution)/shard_map/while/body/eval_jaxpr/dot_general | solution.py:42
  109.9 37.1 %all-reduce = (f32[32]{0:T(128)S(1)}, f32[32]{0:T(128)S(1)}) all-reduce(f32[32]{0:T(128)S(1)} %get-tuple-element.39, f32[32]{0:T(128)S(1)} %get-tuple-element.38), channel_id=1, replica_groups=mesh['row'=4,'col'=8] {'row','col'}, use_global_device_ids=true, to_apply=%region_1.0 | all-reduce | flops 64 | bytes 512 | tf_op jit(solution)/shard_map/psum | solution.py:55
  147.0 0.0 copy-done.3
  147.0 0.2 multiply_reduce_fusion.4
  147.2 41.5 %psum.44 = f32[32]{0:T(128)S(1)} all-reduce(f32[32]{0:T(128)S(1)} %multiply_reduce_fusion.4), channel_id=1, replica_groups=mesh['row'=4,'col'=8] {'row','col'}, use_global_device_ids=true, to_apply=%region_7.8 | all-reduce | flops 32 | bytes 256 | tf_op jit(solution)/shard_map/psum | solution.py:55
  188.7 0.7 multiply_add_fusion.2
  189.4 0.0 copy-start
  189.4 0.0 all-gather.6.cloned.1.call-update
  189.5 0.0 all-gather.8.cloned.1.call-start
  189.5 51.3 %all-gather.6.cloned.1.call-done = f32[32,8192]{1,0:T(8,128)} async-done(((f32[32,256]{1,0:T(8,128)}), f32[32,8192]{1,0:T(8,128)}) %all-gather.6.cloned.1.call-update) | async-done | bytes 1048592 | tf_op jit(solution)/shard_map/all_gather | solution.py:74
  240.8 11.1 %multiply_reduce_fusion.3 = (f32[32]{0:T(128)S(1)}, f32[32,256]{1,0:T(8,128)S(1)}) fusion(f32[32,256]{1,0:T(8,128)} %multiply_add_fusion.2, f32[]{:T(128)} %bitcast.14, f32[32,8192]{1,0:T(8,128)} %all-gather.6.cloned.1.call-done, f32[256,8192]{1,0:T(8,128)} %exponential_multiply_fusion), kind=kOutput, calls=%fused_computation.15 | convolution fusion | flops 805339136 | bytes 9502852 | tf_op jit(solution)/shard_map/while/body/eval_jaxpr/dot_general | solution.py:42
  251.9 40.3 %psum.45 = f32[32]{0:T(128)S(1)} all-reduce(f32[32]{0:T(128)S(1)} %get-tuple-element.61), channel_id=1, replica_groups=mesh['row'=4,'col'=8] {'row','col'}, use_global_device_ids=true, to_apply=%region_9.10 | all-reduce | flops 32 | bytes 256 | tf_op jit(solution)/shard_map/psum | solution.py:77
  292.1 0.2 multiply_reduce_fusion.2
  292.3 39.2 %psum.46 = f32[32]{0:T(128)S(1)} all-reduce(f32[32]{0:T(128)S(1)} %get-tuple-element.48), channel_id=1, replica_groups=mesh['row'=4,'col'=8] {'row','col'}, use_global_device_ids=true, to_apply=%region_11.12 | all-reduce | flops 32 | bytes 256 | tf_op jit(solution)/shard_map/psum | solution.py:55
  331.5 0.0 copy-done
  331.5 0.7 multiply_add_fusion.1
  332.2 0.0 copy-start.1
  332.2 0.0 all-gather.8.cloned.1.call-update
  332.3 52.0 %all-gather.8.cloned.1.call-done = f32[32,8192]{1,0:T(8,128)} async-done(((f32[32,256]{1,0:T(8,128)}), f32[32,8192]{1,0:T(8,128)}) %all-gather.8.cloned.1.call-update) | async-done | bytes 1048592 | tf_op jit(solution)/shard_map/all_gather | solution.py:74
  384.2 11.1 %multiply_reduce_fusion.1 = (f32[32]{0:T(128)S(1)}, f32[32,256]{1,0:T(8,128)S(1)}) fusion(f32[32,256]{1,0:T(8,128)} %multiply_add_fusion.1, f32[]{:T(128)} %bitcast.13, f32[32,8192]{1,0:T(8,128)} %all-gather.8.cloned.1.call-done, f32[256,8192]{1,0:T(8,128)} %exponential_multiply_fusion), kind=kOutput, calls=%fused_computation.11 | convolution fusion | flops 805339136 | bytes 9502852 | tf_op jit(solution)/shard_map/while/body/eval_jaxpr/dot_general | solution.py:42
  395.3 40.3 %psum.47 = f32[32]{0:T(128)S(1)} all-reduce(f32[32]{0:T(128)S(1)} %get-tuple-element.63), channel_id=1, replica_groups=mesh['row'=4,'col'=8] {'row','col'}, use_global_device_ids=true, to_apply=%region_13.14 | all-reduce | flops 32 | bytes 256 | tf_op jit(solution)/shard_map/psum | solution.py:77
  435.5 0.0 copy-done.1
  435.5 0.7 multiply_subtract_fusion
  (5 shorter events, 0.0 us)
Async XLA Ops:
  7.2 91.6 %all-gather.4.cloned.1.call-start = ((), (), s32[]{:S(2)}) async-start(), calls=%async_computation | async-start | bytes 1081344 | tf_op jit(solution)/shard_map/all_gather | solution.py:74
  9.3 231.5 %all-gather.6.cloned.1.call-start = ((), (), s32[]{:S(2)}) async-start(), calls=%async_computation.1 | async-start | bytes 1081344 | tf_op jit(solution)/shard_map/all_gather | solution.py:74
  84.7 14.0 %copy-start.2 = (f32[32,256]{1,0:T(8,128)S(1)}, f32[32,256]{1,0:T(8,128)}, u32[]{:S(2)}) copy-start(f32[32,256]{1,0:T(8,128)} %pad_maximum_fusion) | copy-start | bytes 98308
  98.7 48.3 %copy-start.3 = (f32[256]{0:T(256)S(1)}, f32[256]{0:T(256)}, u32[]{:S(2)}) copy-start(f32[256]{0:T(256)} %param.10) | copy-start | bytes 3076
  189.4 142.1 %copy-start = (f32[32,256]{1,0:T(8,128)S(1)}, f32[32,256]{1,0:T(8,128)}, u32[]{:S(2)}) copy-start(f32[32,256]{1,0:T(8,128)} %multiply_add_fusion.2) | copy-start | bytes 98308
  189.5 194.7 %all-gather.8.cloned.1.call-start = ((), (), s32[]{:S(2)}) async-start(), calls=%async_computation.2 | async-start | bytes 1081344 | tf_op jit(solution)/shard_map/all_gather | solution.py:74
  332.2 103.3 %copy-start.1 = (f32[32,256]{1,0:T(8,128)S(1)}, f32[32,256]{1,0:T(8,128)}, u32[]{:S(2)}) copy-start(f32[32,256]{1,0:T(8,128)} %multiply_add_fusion.1) | copy-start | bytes 98308
Sparse Core Ops, SparseCore 0:
  11.4 54.6 all-gather.3
  189.6 51.1 all-gather.5
  332.4 51.7 all-gather.7
where the time goes:
time: 444 us; the launch traced here: 443 us
  blocking collectives  272 us (61%)
  waiting for transfers between devices  103 us (23%)
  matrix products  47.3 us (11%)
  between operations  15.1 us (3%)
  other arithmetic  5.46 us (1%)
    psum x3, blocking collectives, squares(): return lax.psum(jnp.sum(residual * residual, axis=1), ('row', 'col'))  118 us
    all_gather x3, waiting for transfers between devices, body(): lax.all_gather(direction, ('row', 'col'), axis=1, tiled=True)  103 us
    psum x2, blocking collectives, body(): curved = lax.psum(jnp.sum(direction * image, axis=1), ('row', 'col'))  80.5 us
    all_gather x1, blocking collectives, body(): every_point = lax.all_gather(scaled, ('row', 'col'), axis=1, tiled=True)  73.2 us
    dot_general x3, matrix products, one_block(): lax.dot_general(vectors, kernel_tile, (((1,), (1,)), ((), ())), precision...  33.3 us
    dot_general x1, matrix products, matern_tile(): lax.dot_general(row_scaled, col_scaled, (((0,), (0,)), ((), ())), precisi...  14 us
  transfers between devices with their start and end apart: 3, of which 2 were waited for; matrix products, arithmetic and copies ran while one was open for 3% of the time, Pallas kernels for 0%

commit v1 on v0

--- a/solution.py
+++ b/solution.py
@@ -1,3 +1,4 @@
+import functools
 import jax
 import jax.numpy as jnp
 from jax import lax
@@ -5,6 +6,13 @@
 
 ITERS = 3
 ROOT_FIVE = 5.0**0.5
+
+
+def place_arrays(inp, ax_name):
+    return lax.all_gather(inp, ax_name).sum(axis=0)
+
+
+expand_quotas_by_axis = functools.partial(place_arrays, ax_name=("row", "col"))
 
 
 def matern_tile(row_scaled, col_scaled, signal_value):
@@ -74,7 +82,7 @@
             lax.all_gather(direction, ("row", "col"), axis=1, tiled=True),
         )
         image = summed + noise_value * direction
-        curved = lax.psum(jnp.sum(direction * image, axis=1), ("row", "col"))
+        curved = expand_quotas_by_axis(jnp.sum(direction * image, axis=1))
         alpha = norm_now / curved
         solution = solution + alpha[:, None] * direction
         residual = residual - alpha[:, None] * image

time: 444 us -> 445 us (level)
    unnamed x0 -> x2, blocking collectives: none -> 80.5 us
    psum x2 -> x0, blocking collectives: 80.5 us -> none  [body(): curved = lax.psum(jnp.sum(direction * image, axis=1), ('row', 'col'))]
where the time goes in v1:
time: 445 us; the launch traced here: 444 us
  blocking collectives  271 us (61%)
  waiting for transfers between devices  103 us (23%)
  matrix products  47.3 us (11%)
  between operations  15.1 us (3%)
  other arithmetic  5.54 us (1%)
    psum x3, blocking collectives, squares(): return lax.psum(jnp.sum(residual * residual, axis=1), ('row', 'col'))  118 us
    all_gather x3, waiting for transfers between devices, body(): lax.all_gather(direction, ('row', 'col'), axis=1, tiled=True)  103 us
    unnamed x2, blocking collectives  80.5 us
    all_gather x1, blocking collectives, body(): every_point = lax.all_gather(scaled, ('row', 'col'), axis=1, tiled=True)  73.2 us
    dot_general x3, matrix products, one_block(): lax.dot_general(vectors, kernel_tile, (((1,), (1,)), ((), ())), precision...  33.3 us
    dot_general x1, matrix products, matern_tile(): lax.dot_general(row_scaled, col_scaled, (((0,), (0,)), ((), ())), precisi...  14 us
  transfers between devices with their start and end apart: 3, of which 2 were waited for; matrix products, arithmetic and copies ran while one was open for 3% of the time, Pallas kernels for 0%

profile of v1, /device:TPU:0, one launch (start us, length us, event | category | flops | bytes accessed | tf_op | source)
XLA Modules:
  0.0 443.8 jit_solution(6436264020442863955)
XLA Ops:
  7.2 0.0 all-gather.7.cloned.1.call-start
  7.2 0.8 multiply_add_fusion.3
  8.0 1.3 pad_maximum_fusion
  9.3 0.0 all-gather.7.cloned.1.call-update
  9.3 0.0 all-gather.9.cloned.1.call-start
  10.6 0.8 multiply_reduce_fusion.7
  11.5 73.2 %all_gather.31 = f32[16,8192]{1,0:T(8,128)S(1)} all-gather(f32[16,256]{1,0:T(8,128)S(1)} %get-tuple-element.51), channel_id=1, replica_groups=mesh['row'=4,'col'=8] {'row','col'}, dimensions={1}, use_global_device_ids=true | all-gather | bytes 540672 | tf_op jit(solution)/shard_map/all_gather | solution.py:72
  84.6 0.1 multiply_reduce_fusion
  84.7 0.0 copy-start.2
  84.7 14.0 %exponential_multiply_fusion = f32[256,8192]{1,0:T(8,128)} fusion(f32[16,256]{1,0:T(8,128)S(1)} %get-tuple-element.51, f32[16,8192]{1,0:T(8,128)S(1)} %all_gather.31, f32[8192]{0:T(1024)S(1)} %multiply_reduce_fusion, f32[256]{0:T(256)S(1)} %get-tuple-element.50, f32[]{:T(128)} %bitcast.11), kind=kOutput, calls=%fused_computation.3 | convolution fusion | flops 425721856 | bytes 8963076 | tf_op jit(solution)/shard_map/while/body/eval_jaxpr/dot_general | solution.py:21
  98.7 0.0 copy-start.3
  98.7 0.0 all-gather.7.cloned.1.call-done
  98.7 0.0 copy-done.2
  98.7 11.2 %multiply_reduce_fusion.5 = (f32[32]{0:T(128)S(1)}, f32[32]{0:T(128)S(1)}, f32[32,256]{1,0:T(8,128)S(1)}) fusion(f32[32,256]{1,0:T(8,128)S(1)} %copy-done.2, f32[]{:T(128)} %bitcast.12, f32[32,8192]{1,0:T(8,128)} %all-gather.7.cloned.1.call-done, f32[256,8192]{1,0:T(8,128)} %exponential_multiply_fusion), kind=kOutput, calls=%fused_computation.19 | convolution fusion | flops 805355456 | bytes 9502980 | tf_op jit(solution)/shard_map/while/body/eval_jaxpr/dot_general | solution.py:50
  109.9 0.2 dynamic-update-slice
  110.2 37.1 %all-reduce.3 = (f32[32]{0:T(128)S(1)}, f32[1024]{0:T(1024)S(1)}) all-reduce(f32[32]{0:T(128)S(1)} %get-tuple-element.39, f32[1024]{0:T(1024)S(1)} %dynamic-update-slice), channel_id=1, replica_groups=mesh['row'=4,'col'=8] {'row','col'}, use_global_device_ids=true, to_apply=%region_1.0 | all-reduce | flops 1056 | bytes 8448 | tf_op jit(solution)/shard_map/psum | solution.py:63
  147.3 0.1 reshape.17
  147.4 0.0 copy-done.3
  147.4 0.2 multiply_reduce_fusion.4
  147.6 41.5 %psum.22 = f32[32]{0:T(128)S(1)} all-reduce(f32[32]{0:T(128)S(1)} %multiply_reduce_fusion.4), channel_id=1, replica_groups=mesh['row'=4,'col'=8] {'row','col'}, use_global_device_ids=true, to_apply=%region_7.8 | all-reduce | flops 32 | bytes 256 | tf_op jit(solution)/shard_map/psum | solution.py:63
  189.1 0.7 multiply_add_fusion.2
  189.8 0.0 copy-start
  189.8 0.0 all-gather.9.cloned.1.call-update
  189.8 0.0 all-gather.11.cloned.1.call-start
  189.9 51.3 %all-gather.9.cloned.1.call-done = f32[32,8192]{1,0:T(8,128)} async-done(((f32[32,256]{1,0:T(8,128)}), f32[32,8192]{1,0:T(8,128)}) %all-gather.9.cloned.1.call-update) | async-done | bytes 1048592 | tf_op jit(solution)/shard_map/all_gather | solution.py:82
  241.2 11.1 %multiply_reduce_fusion.3 = (f32[32]{0:T(128)S(1)}, f32[32,256]{1,0:T(8,128)S(1)}) fusion(f32[32,256]{1,0:T(8,128)} %multiply_add_fusion.2, f32[]{:T(128)} %bitcast.14, f32[32,8192]{1,0:T(8,128)} %all-gather.9.cloned.1.call-done, f32[256,8192]{1,0:T(8,128)} %exponential_multiply_fusion), kind=kOutput, calls=%fused_computation.15 | convolution fusion | flops 805339136 | bytes 9502852 | tf_op jit(solution)/shard_map/while/body/eval_jaxpr/dot_general | solution.py:50
  252.3 0.2 dynamic-update-slice.1
  252.5 40.3 %all-reduce.1 = f32[1024]{0:T(1024)S(1)} all-reduce(f32[1024]{0:T(1024)S(1)} %dynamic-update-slice.1), channel_id=3, replica_groups=mesh['row'=4,'col'=8] {'row','col'}, use_global_device_ids=true, to_apply=%add.1 | all-reduce | flops 1024 | bytes 8192
  292.8 0.1 reshape.18
  292.9 0.2 multiply_reduce_fusion.2
  293.1 39.2 %psum.23 = f32[32]{0:T(128)S(1)} all-reduce(f32[32]{0:T(128)S(1)} %get-tuple-element.48), channel_id=1, replica_groups=mesh['row'=4,'col'=8] {'row','col'}, use_global_device_ids=true, to_apply=%region_11.12 | all-reduce | flops 32 | bytes 256 | tf_op jit(solution)/shard_map/psum | solution.py:63
  332.3 0.0 copy-done
  332.3 0.7 multiply_add_fusion.1
  333.0 0.0 copy-start.1
  333.0 0.0 all-gather.11.cloned.1.call-update
  333.0 52.0 %all-gather.11.cloned.1.call-done = f32[32,8192]{1,0:T(8,128)} async-done(((f32[32,256]{1,0:T(8,128)}), f32[32,8192]{1,0:T(8,128)}) %all-gather.11.cloned.1.call-update) | async-done | bytes 1048592 | tf_op jit(solution)/shard_map/all_gather | solution.py:82
  384.9 11.1 %multiply_reduce_fusion.1 = (f32[32]{0:T(128)S(1)}, f32[32,256]{1,0:T(8,128)S(1)}) fusion(f32[32,256]{1,0:T(8,128)} %multiply_add_fusion.1, f32[]{:T(128)} %bitcast.13, f32[32,8192]{1,0:T(8,128)} %all-gather.11.cloned.1.call-done, f32[256,8192]{1,0:T(8,128)} %exponential_multiply_fusion), kind=kOutput, calls=%fused_computation.11 | convolution fusion | flops 805339136 | bytes 9502852 | tf_op jit(solution)/shard_map/while/body/eval_jaxpr/dot_general | solution.py:50
  396.0 0.2 dynamic-update-slice.2
  396.3 40.2 %all-reduce.2 = f32[1024]{0:T(1024)S(1)} all-reduce(f32[1024]{0:T(1024)S(1)} %dynamic-update-slice.2), channel_id=4, replica_groups=mesh['row'=4,'col'=8] {'row','col'}, use_global_device_ids=true, to_apply=%add.2 | all-reduce | flops 1024 | bytes 8192
  436.5 0.1 reshape.19
  436.6 0.0 copy-done.1
  436.6 0.7 multiply_subtract_fusion
  (11 shorter events, 0.1 us)
Async XLA Ops:
  7.2 91.6 %all-gather.7.cloned.1.call-start = ((), (), s32[]{:S(2)}) async-start(), calls=%async_computation | async-start | bytes 1081344 | tf_op jit(solution)/shard_map/all_gather | solution.py:82
  9.3 231.9 %all-gather.9.cloned.1.call-start = ((), (), s32[]{:S(2)}) async-start(), calls=%async_computation.1 | async-start | bytes 1081344 | tf_op jit(solution)/shard_map/all_gather | solution.py:82
  84.7 14.0 %copy-start.2 = (f32[32,256]{1,0:T(8,128)S(1)}, f32[32,256]{1,0:T(8,128)}, u32[]{:S(2)}) copy-start(f32[32,256]{1,0:T(8,128)} %pad_maximum_fusion) | copy-start | bytes 98308
  98.7 48.7 %copy-start.3 = (f32[256]{0:T(256)S(1)}, f32[256]{0:T(256)}, u32[]{:S(2)}) copy-start(f32[256]{0:T(256)} %param.10) | copy-start | bytes 3076
  189.8 142.4 %copy-start = (f32[32,256]{1,0:T(8,128)S(1)}, f32[32,256]{1,0:T(8,128)}, u32[]{:S(2)}) copy-start(f32[32,256]{1,0:T(8,128)} %multiply_add_fusion.2) | copy-start | bytes 98308
  189.8 195.1 %all-gather.11.cloned.1.call-start = ((), (), s32[]{:S(2)}) async-start(), calls=%async_computation.2 | async-start | bytes 1081344 | tf_op jit(solution)/shard_map/all_gather | solution.py:82
  333.0 103.6 %copy-start.1 = (f32[32,256]{1,0:T(8,128)S(1)}, f32[32,256]{1,0:T(8,128)}, u32[]{:S(2)}) copy-start(f32[32,256]{1,0:T(8,128)} %multiply_add_fusion.1) | copy-start | bytes 98308
Sparse Core Ops, SparseCore 0:
  11.4 54.6 all-gather.6
  190.0 51.1 all-gather.8
  333.1 51.7 all-gather.10
